TPU v7x, 32 devices: a whole 2x2x4 slice. The times are simulated.
32 devices in a mesh: cells: 8 (over z, y), bins: 4 (over x, core).
Axes of the slice: x: 2, y: 2, z: 4, core: 2. Of those that a mesh axis runs over, the one named last changes fastest.
Arguments:
- snapshots: bfloat16 [4, 65536, 512], P('bins', 'cells'), may hold values from -150 to 150
- training: int32 [65536], P('cells'), may hold values 0 or 1
- doppler: int32 [4, 128], P('bins'), may hold values from 0 to 1023
Outputs:
- filtered: bfloat16 [4, 256, 65536], P('bins', None, 'cells')
All inputs are finite; a program needn't handle non-finite values. No bound on the sum of `training` on one device may be relied on, other than what follows from the above.
Results may differ from a plain program's by a relative error of at most 0.003.
The roundings to bfloat16 on the way count: a program that leaves them out, or rounds other values in their place, can miss the bound.
Values sent between devices are 32-bit elements; how exact they have to be, the bound alone decides.
A program may use at most 64 MiB of HBM per device.

v0:
```python
import functools

import jax
import jax.numpy as jnp
from jax import lax
from jax.experimental import pallas as pl
from jax.experimental.pallas import tpu as pltpu
from jax.sharding import PartitionSpec as P

CHANNELS = 16
PULSES = 16
NDOPP = 1024


load_ratio = 0.5
look_freq = 0.125

EXTRA = 8
DONE = 0.99
REFINE = 2
HIGH = lax.Precision.HIGH
HIGHEST = lax.Precision.HIGHEST
MESH = pl.DeviceIdType.MESH


def steering(doppler, chans, pulses):
    index = jnp.arange(chans * pulses)
    chan = (index // pulses).astype(jnp.float32)
    pulse = (index % pulses).astype(jnp.float32)
    freq = doppler.astype(jnp.float32) / NDOPP - 0.5
    phase = 2.0 * jnp.pi * (look_freq * chan[:, None] + pulse[:, None] * freq[None, :])
    return jnp.concatenate([jnp.cos(phase), jnp.sin(phase)], 0) / jnp.sqrt(
        jnp.float32(chans * pulses)
    )


def gram_kernel(half, x_ref, keep_ref, out_ref, real_sum, cross_sum):
    step = pl.program_id(0)

    @pl.when(step == 0)
    def _():
        real_sum[...] = jnp.zeros_like(real_sum)
        cross_sum[...] = jnp.zeros_like(cross_sum)

    x = x_ref[...]
    keep = keep_ref[...].astype(jnp.bfloat16)
    masked = x.T * keep
    mr, mi = masked[:half], masked[half:]
    r, i = x[:, :half], x[:, half:]
    real_sum[...] += jnp.dot(
        jnp.concatenate([mr, mi], 1),
        jnp.concatenate([r, i], 0),
        preferred_element_type=jnp.float32,
    )
    cross_sum[...] += jnp.dot(mr, i, preferred_element_type=jnp.float32)

    @pl.when(step == pl.num_programs(0) - 1)
    def _():
        real = real_sum[...]
        cross = cross_sum[...]
        rows = lax.broadcasted_iota(jnp.int32, (half, half), 0)
        cols = lax.broadcasted_iota(jnp.int32, (half, half), 1)
        out_ref[...] = jnp.where(rows <= cols, real, cross.T - cross)


def gram(snaps, keep, block):
    cells, width = snaps.shape
    half = width // 2
    return pl.pallas_call(
        functools.partial(gram_kernel, half),
        grid=(cells // block,),
        in_specs=[
            pl.BlockSpec((block, width), lambda i: (i, 0)),
            pl.BlockSpec((1, block), lambda i: (0, i)),
        ],
        out_specs=pl.BlockSpec((half, half), lambda i: (0, 0)),
        out_shape=jax.ShapeDtypeStruct((half, half), jnp.float32),
        scratch_shapes=[
            pltpu.VMEM((half, half), jnp.float32),
            pltpu.VMEM((half, half), jnp.float32),
        ],
        name="gram",
    )(snaps, keep)


def sum_kernel(n, m, x_ref, out_ref, rs_buf, tr_src, tr_buf, mine, sems):
    me = lax.axis_index("cells")
    g = lax.axis_index("bins")
    half = x_ref.shape[0]
    rows = half // n
    rs_send, rs_recv, tr_send, tr_recv, ag_send, ag_recv = sems

    barrier = pltpu.get_barrier_semaphore()
    for k in range(1, n):
        pl.semaphore_signal(
            barrier, inc=1, device_id=(lax.rem(me + k, n), g), device_id_type=MESH
        )
    for k in range(1, m):
        pl.semaphore_signal(
            barrier, inc=1, device_id=(me, lax.rem(g + k, m)), device_id_type=MESH
        )
    pl.semaphore_wait(barrier, n + m - 2)

    copies = []
    for k in range(1, n):
        peer = lax.rem(me + k, n)
        copy = pltpu.make_async_remote_copy(
            src_ref=x_ref.at[pl.ds(pl.multiple_of(peer * rows, rows), rows)],
            dst_ref=rs_buf.at[k - 1],
            send_sem=rs_send.at[k - 1],
            recv_sem=rs_recv.at[k - 1],
            device_id=(peer, g),
            device_id_type=MESH,
        )
        copy.start()
        copies.append(copy)
    r = lax.broadcasted_iota(jnp.int32, (half, half), 0)
    c = lax.broadcasted_iota(jnp.int32, (half, half), 1)
    trace = jnp.sum(jnp.where(r == c, x_ref[...], 0.0), axis=0, keepdims=True)
    tr_src[...] = jnp.broadcast_to(trace, tr_src.shape)
    for k in range(1, m):
        copy = pltpu.make_async_remote_copy(
            src_ref=tr_src,
            dst_ref=tr_buf.at[k - 1],
            send_sem=tr_send.at[k - 1],
            recv_sem=tr_recv.at[k - 1],
            device_id=(me, lax.rem(g + k, m)),
            device_id_type=MESH,
        )
        copy.start()
        copies.append(copy)
    for copy in copies:
        copy.wait()
    total = x_ref[pl.ds(pl.multiple_of(me * rows, rows), rows), :]
    for k in range(n - 1):
        total = total + rs_buf[k]
    power = tr_src[...]
    for k in range(m - 1):
        power = power + tr_buf[k]
    mine[pl.ds(0, rows), :] = total
    mine[pl.ds(rows, EXTRA), :] = power
    out_ref[me] = jnp.concatenate([total, power], 0)

    copies = []
    for k in range(1, n):
        copy = pltpu.make_async_remote_copy(
            src_ref=mine,
            dst_ref=out_ref.at[me],
            send_sem=ag_send.at[k - 1],
            recv_sem=ag_recv.at[k - 1],
            device_id=(lax.rem(me + k, n), g),
            device_id_type=MESH,
        )
        copy.start()
        copies.append(copy)
    for k in range(1, n):
        copies[k - 1].wait_send()
        pltpu.make_async_remote_copy(
            src_ref=mine,
            dst_ref=out_ref.at[lax.rem(me + n - k, n)],
            send_sem=ag_send.at[k - 1],
            recv_sem=ag_recv.at[k - 1],
            device_id=(lax.rem(me + n - k, n), g),
            device_id_type=MESH,
        ).wait_recv()


def all_sum(packed):
    n, m = lax.axis_size("cells"), lax.axis_size("bins")
    half = packed.shape[0]
    rows = half // n
    dma = pltpu.SemaphoreType.DMA
    return pl.pallas_call(
        functools.partial(sum_kernel, n, m),
        out_shape=jax.ShapeDtypeStruct((n, rows + EXTRA, half), jnp.float32),
        in_specs=[pl.BlockSpec(memory_space=pltpu.VMEM)],
        out_specs=pl.BlockSpec(memory_space=pltpu.VMEM),
        scratch_shapes=[
            pltpu.VMEM((n - 1, rows, half), jnp.float32),
            pltpu.VMEM((EXTRA, half), jnp.float32),
            pltpu.VMEM((m - 1, EXTRA, half), jnp.float32),
            pltpu.VMEM((rows + EXTRA, half), jnp.float32),
            [dma((n - 1,)), dma((n - 1,)), dma((m - 1,)), dma((m - 1,)), dma((n - 1,)), dma((n - 1,))],
        ],
        compiler_params=pltpu.CompilerParams(collective_id=0, has_side_effects=True),
        name="all_sum",
    )(packed)


def newton_steps(ratio):
    d, steps = 1.0 / (ratio + 1.0), 0
    while d < DONE:
        d = (4.0 * d - 2.0 * d * d) / (1.0 + 2.0 * d - d * d)
        steps += 1
    return steps - 1


def solve_kernel(groups, parts_ref, steer_ref, taps_ref, mat, full, col):
    n = parts_ref.shape[0]
    rows = parts_ref.shape[1] - EXTRA
    half = parts_ref.shape[2]
    summed = jnp.concatenate([parts_ref[k, :rows, :] for k in range(n)], 0)
    power_row = parts_ref[0, rows:rows + 1, :]
    for k in range(1, n):
        power_row = power_row + parts_ref[k, rows:rows + 1, :]
    noise = jnp.sum(power_row, axis=1, keepdims=True) / (groups * half)
    low = load_ratio * noise
    r = lax.broadcasted_iota(jnp.int32, (half, half), 0)
    c = lax.broadcasted_iota(jnp.int32, (half, half), 1)
    flip = summed.T
    trace = jnp.sum(
        jnp.sum(jnp.where(r == c, summed, 0.0), axis=0, keepdims=True), axis=1, keepdims=True
    )
    eye = jnp.where(r == c, 1.0, 0.0)
    scale = 1.0 / (0.5 * trace + low)
    real = (jnp.where(r <= c, summed, flip) + low * eye) * scale
    imag = jnp.where(r > c, summed, jnp.where(r < c, -flip, 0.0)) * scale
    mat[:half, :half] = real
    mat[half:, half:] = real
    mat[:half, half:] = -imag
    mat[half:, :half] = imag

    def put(xr, xi):
        col[:half, :] = xr
        col[half:, :] = xi
        full[:half, :half] = xr
        full[half:, half:] = xr
        full[:half, half:] = -xi
        full[half:, :half] = xi

    d = low * scale
    bend = 2.0 / (1.0 + 2.0 * d - d * d)
    d = (4.0 * d - 2.0 * d * d) / (1.0 + 2.0 * d - d * d)
    put(bend * (2.0 * eye - real), -bend * imag)

    def newton(_, d):
        left = jnp.dot(mat[...], col[...], preferred_element_type=jnp.float32, precision=HIGH)
        bend = 2.0 / (1.0 + 2.0 * d - d * d)
        step = jnp.dot(
            full[...],
            jnp.concatenate([2.0 * eye - left[:half], -left[half:]], 0),
            preferred_element_type=jnp.float32,
            precision=HIGH,
        )
        put(bend * step[:half], bend * step[half:])
        return (4.0 * d - 2.0 * d * d) / (1.0 + 2.0 * d - d * d)

    lax.fori_loop(0, newton_steps(groups * half), newton, d)

    steer = steer_ref[...]
    w = jnp.dot(full[...], steer, preferred_element_type=jnp.float32, precision=HIGH)
    for _ in range(REFINE):
        gap = steer - jnp.dot(mat[...], w, preferred_element_type=jnp.float32, precision=HIGHEST)
        w = w + jnp.dot(full[...], gap, preferred_element_type=jnp.float32, precision=HIGH)
    w = w * scale
    gain = jnp.sum(steer * w, axis=0, keepdims=True)
    wr = (w[:half] / gain).T
    wi = (w[half:] / gain).T
    bins = wr.shape[0]
    taps_ref[:bins, :half] = wr.astype(jnp.bfloat16)
    taps_ref[:bins, half:] = wi.astype(jnp.bfloat16)
    taps_ref[bins:, :half] = (-wi).astype(jnp.bfloat16)
    taps_ref[bins:, half:] = wr.astype(jnp.bfloat16)


def solve(parts, steer, groups):
    half = parts.shape[2]
    bins = steer.shape[1]
    return pl.pallas_call(
        functools.partial(solve_kernel, groups),
        out_shape=jax.ShapeDtypeStruct((2 * bins, 2 * half), jnp.bfloat16),
        in_specs=[pl.BlockSpec(memory_space=pltpu.VMEM)] * 2,
        out_specs=pl.BlockSpec(memory_space=pltpu.VMEM),
        scratch_shapes=[
            pltpu.VMEM((2 * half, 2 * half), jnp.float32),
            pltpu.VMEM((2 * half, 2 * half), jnp.float32),
            pltpu.VMEM((2 * half, half), jnp.float32),
        ],
        name="solve",
    )(parts, steer)


def filter_kernel(taps_ref, x_ref, out_ref):
    out_ref[...] = lax.dot_general(
        taps_ref[...], x_ref[...], (((1,), (1,)), ((), ())), preferred_element_type=jnp.float32
    ).astype(out_ref.dtype)


def apply_taps(taps, snaps, block):
    cells, width = snaps.shape
    rows = taps.shape[0]
    return pl.pallas_call(
        filter_kernel,
        grid=(cells // block,),
        in_specs=[
            pl.BlockSpec((rows, width), lambda i: (0, 0)),
            pl.BlockSpec((block, width), lambda i: (i, 0)),
        ],
        out_specs=pl.BlockSpec((rows, block), lambda i: (0, i)),
        out_shape=jax.ShapeDtypeStruct((rows, cells), jnp.bfloat16),
        name="filter",
    )(taps, snaps)


def per_device(snapshots, training, doppler):
    snaps = snapshots[0]
    block = min(4096, snaps.shape[0])
    packed = gram(snaps, training[None, :], block)
    parts = all_sum(packed)
    steer = steering(doppler[0], CHANNELS, PULSES)
    taps = solve(parts, steer, lax.axis_size("bins"))
    return apply_taps(taps, snaps, block)[None]


def solution(mesh):
    in_specs = (P("bins", "cells", None), P("cells"), P("bins", None))
    out_specs = P("bins", None, "cells")
    return jax.shard_map(
        per_device, mesh=mesh, in_specs=in_specs, out_specs=out_specs, check_vma=False
    )
```

profile of v0, /device:TPU:0, one launch (start us, length us, event | category | flops | bytes accessed | tf_op | source)
XLA Modules:
  0.0 53.8 jit_solution(9880492106443107611)
XLA Ops:
  0.0 0.7 %add_bitcast_fusion = f32[128]{0:T(128)S(1)} fusion(s32[1,128]{1,0:T(1,128)} %param.5), kind=kLoop, calls=%fused_computation.14 | loop fusion | flops 384 | bytes 1024 | tf_op jit(solution)/shard_map/mul | solution.py:31
  0.7 0.6 %fusion.1 = (f32[256,128]{1,0:T(8,128)S(1)}, f32[256,128]{1,0:T(8,128)S(1)}) fusion(f32[128]{0:T(128)S(1)} %add_bitcast_fusion, f32[256]{0:T(256)S(1)} %fusion.4, f32[256]{0:T(256)S(1)} %fusion.6), kind=kLoop, calls=%fused_computation.3 | loop fusion | flops 98304 | bytes 264704 | tf_op jit(solution)/shard_map/cos | solution.py:32
  1.3 0.7 %maximum_multiply_fusion.steer_ref = f32[512,128]{1,0:T(8,128)} fusion(f32[256,128]{1,0:T(8,128)S(1)} %get-tuple-element.6, f32[256,128]{1,0:T(8,128)S(1)} %get-tuple-element.5), kind=kLoop, calls=%fused_computation | loop fusion | flops 131072 | bytes 524288 | tf_op jit(solution)/shard_map/div | solution.py:32
  2.0 6.7 %gram.1.x_ref = f32[256,256]{1,0:T(8,128)} custom-call(bf16[8192,512]{1,0:T(8,128)(2,1)} %bitcast.5, s32[1,8192]{1,0:T(1,128)} %bitcast.7), custom_call_target="tpu_custom_call" | custom-call | tf_op jit(solution)/shard_map/gram/pallas_call | solution.py:69
  8.7 20.2 %all_sum.1.parts_ref = f32[8,40,256]{2,1,0:T(8,128)} custom-call(f32[256,256]{1,0:T(8,128)} %gram.1.x_ref), custom_call_target="tpu_custom_call" | custom-call | tf_op jit(solution)/shard_map/all_sum/pallas_call | solution.py:173
  28.9 18.8 %solve.1.taps_ref = bf16[256,512]{1,0:T(8,128)(2,1)} custom-call(f32[8,40,256]{2,1,0:T(8,128)} %all_sum.1.parts_ref, f32[512,128]{1,0:T(8,128)} %maximum_multiply_fusion.steer_ref), custom_call_target="tpu_custom_call" | custom-call | tf_op jit(solution)/shard_map/solve/pallas_call | solution.py:269
  47.7 6.2 %filter.1 = bf16[256,8192]{1,0:T(8,128)(2,1)} custom-call(bf16[256,512]{1,0:T(8,128)(2,1)} %solve.1.taps_ref, bf16[8192,512]{1,0:T(8,128)(2,1)} %bitcast.6), custom_call_target="tpu_custom_call" | custom-call | tf_op jit(solution)/shard_map/filter/pallas_call | solution.py:292
  (2 shorter events, 0.0 us)
where the time goes:
time: 54.7 us; the launch traced here: 53.8 us
  Pallas kernels  51.9 us (95%)
  other arithmetic  1.97 us (4%)
    pallas_call x1, Pallas kernels, all_sum(): pl.pallas_call(functools.partial(sum_kernel, n, m), out_shape=jax.ShapeDt...  20.2 us
    pallas_call x1, Pallas kernels, solve(): pl.pallas_call(functools.partial(solve_kernel, groups), out_shape=jax.Sha...  18.8 us
    pallas_call x1, Pallas kernels, gram(): pl.pallas_call(functools.partial(gram_kernel, half), grid=(cells // block...  6.75 us
    pallas_call x1, Pallas kernels, apply_taps(): pl.pallas_call(filter_kernel, grid=(cells // block,), in_specs=[pl.BlockS...  6.15 us

commit v1 on v0

--- a/solution.py
+++ b/solution.py
@@ -1,4 +1,5 @@
 import functools
+import math
 
 import jax
 import jax.numpy as jnp
@@ -16,22 +17,8 @@
 look_freq = 0.125
 
 EXTRA = 8
-DONE = 0.99
-REFINE = 2
 HIGH = lax.Precision.HIGH
-HIGHEST = lax.Precision.HIGHEST
 MESH = pl.DeviceIdType.MESH
-
-
-def steering(doppler, chans, pulses):
-    index = jnp.arange(chans * pulses)
-    chan = (index // pulses).astype(jnp.float32)
-    pulse = (index % pulses).astype(jnp.float32)
-    freq = doppler.astype(jnp.float32) / NDOPP - 0.5
-    phase = 2.0 * jnp.pi * (look_freq * chan[:, None] + pulse[:, None] * freq[None, :])
-    return jnp.concatenate([jnp.cos(phase), jnp.sin(phase)], 0) / jnp.sqrt(
-        jnp.float32(chans * pulses)
-    )
 
 
 def gram_kernel(half, x_ref, keep_ref, out_ref, real_sum, cross_sum):
@@ -187,18 +174,85 @@
     )(packed)
 
 
-def newton_steps(ratio):
-    d, steps = 1.0 / (ratio + 1.0), 0
-    while d < DONE:
-        d = (4.0 * d - 2.0 * d * d) / (1.0 + 2.0 * d - d * d)
-        steps += 1
-    return steps - 1
-
-
-def solve_kernel(groups, parts_ref, steer_ref, taps_ref, mat, full, col):
+def grow(d):
+    return (4.0 * d - 2.0 * d * d) / (1.0 + 2.0 * d - d * d)
+
+
+def start_for(steps, goal):
+    lo, hi = 0.0, 1.0
+    for _ in range(100):
+        mid = 0.5 * (lo + hi)
+        d = mid
+        for _ in range(steps):
+            d = grow(d)
+        lo, hi = (lo, mid) if d >= goal else (mid, hi)
+    return hi
+
+
+def split(x, parts):
+    out = []
+    for _ in range(parts):
+        top = x.astype(jnp.bfloat16)
+        out.append(top)
+        x = x - top.astype(jnp.float32)
+    return out
+
+
+def mxu(a, b):
+    return jnp.dot(a, b, preferred_element_type=jnp.float32)
+
+
+def total(x):
+    return jnp.sum(jnp.sum(x, axis=0, keepdims=True), axis=1, keepdims=True)
+
+
+def steer_rows(doppler, chans, pulses):
+    bins, dim = doppler.shape[0], chans * pulses
+    index = lax.broadcasted_iota(jnp.int32, (1, dim), 1)
+    pulse = lax.rem(index, pulses)
+    chan = ((index - pulse) // pulses).astype(jnp.float32)
+    freq = doppler.astype(jnp.float32) * (1.0 / NDOPP) - 0.5
+    turns = look_freq * chan + pulse.astype(jnp.float32) * freq
+    phase = (2.0 * math.pi) * turns
+    quarter = jnp.floor(4.0 * turns + 0.5)
+    rest = phase - quarter * 1.5703125
+    rest = rest - quarter * 4.837512969970703125e-4
+    rest = rest - quarter * 7.549789948768648e-8
+    sq = rest * rest
+    sin = rest + rest * sq * (
+        -1.6666654611e-1 + sq * (8.3321608736e-3 + sq * -1.9515295891e-4)
+    )
+    cos = 1.0 + sq * (
+        -0.5 + sq * (4.166664568298827e-2 + sq * (-1.388731625493765e-3 + sq * 2.443315711809948e-5))
+    )
+    which = quarter.astype(jnp.int32) & 3
+    odd = (which & 1) == 1
+    c = jnp.where(odd, sin, cos)
+    s = jnp.where(odd, cos, sin)
+    c = jnp.where((which == 1) | (which == 2), -c, c)
+    s = jnp.where(which >= 2, -s, s)
+    return jnp.concatenate([c, s], 1) * (1.0 / math.sqrt(dim))
+
+
+def solve_kernel(
+    groups, block, parts_ref, dop_ref, x_hbm, out_hbm,
+    x_buf, out_buf, taps, e0, e1, e2, low_mat, low_pair, pair, xs, ys, acol, steer, w_ref, in_sems, out_sems,
+):
     n = parts_ref.shape[0]
     rows = parts_ref.shape[1] - EXTRA
     half = parts_ref.shape[2]
+    full = 2 * half
+    bins = dop_ref.shape[0]
+    cells = x_buf.shape[0]
+    f32, bf16 = jnp.float32, jnp.bfloat16
+
+    loads = []
+    for k in range(cells // block):
+        span = pl.ds(k * block, block)
+        copy = pltpu.make_async_copy(x_hbm.at[span], x_buf.at[span], in_sems.at[k])
+        copy.start()
+        loads.append(copy)
+
     summed = jnp.concatenate([parts_ref[k, :rows, :] for k in range(n)], 0)
     power_row = parts_ref[0, rows:rows + 1, :]
     for k in range(1, n):
@@ -207,99 +261,184 @@
     low = load_ratio * noise
     r = lax.broadcasted_iota(jnp.int32, (half, half), 0)
     c = lax.broadcasted_iota(jnp.int32, (half, half), 1)
+    diag = jnp.where(r == c, summed, 0.0)
+    trace = total(diag)
+    unit = 1.0 / (trace + low)
+    norm = summed * unit
+    fro = jnp.sqrt(total(2.0 * norm * norm - jnp.where(r == c, norm * norm, 0.0))) * (trace + low)
+    bound = jnp.minimum(trace, 1.0001 * fro)
+    scale = 2.0 / (bound + 2.0 * low)
+    eye = jnp.where(r == c, 1.0, 0.0)
     flip = summed.T
-    trace = jnp.sum(
-        jnp.sum(jnp.where(r == c, summed, 0.0), axis=0, keepdims=True), axis=1, keepdims=True
-    )
-    eye = jnp.where(r == c, 1.0, 0.0)
-    scale = 1.0 / (0.5 * trace + low)
     real = (jnp.where(r <= c, summed, flip) + low * eye) * scale
     imag = jnp.where(r > c, summed, jnp.where(r < c, -flip, 0.0)) * scale
-    mat[:half, :half] = real
-    mat[half:, half:] = real
-    mat[:half, half:] = -imag
-    mat[half:, :half] = imag
-
-    def put(xr, xi):
-        col[:half, :] = xr
-        col[half:, :] = xi
-        full[:half, :half] = xr
-        full[half:, half:] = xr
-        full[:half, half:] = -xi
-        full[half:, :half] = xi
-
-    d = low * scale
-    bend = 2.0 / (1.0 + 2.0 * d - d * d)
-    d = (4.0 * d - 2.0 * d * d) / (1.0 + 2.0 * d - d * d)
-    put(bend * (2.0 * eye - real), -bend * imag)
-
-    def newton(_, d):
-        left = jnp.dot(mat[...], col[...], preferred_element_type=jnp.float32, precision=HIGH)
+    acol[:half, :] = real
+    acol[half:, :] = imag
+
+    def quads(ref, base, xr, xi):
+        ref[pl.ds(base, half), :half] = xr
+        ref[pl.ds(base + half, half), half:] = xr
+        ref[pl.ds(base, half), half:] = -xi
+        ref[pl.ds(base + half, half), :half] = xi
+
+    for ref, xr, xi in zip((e0, e1, e2), split(real, 3), split(imag, 3)):
+        quads(ref, 0, xr, xi)
+    steer[...] = steer_rows(dop_ref[...], CHANNELS, PULSES)
+
+    square = mxu(e0[...], e0[:, :half])
+    top = total(square * square)
+    lam = 1.005 * jnp.sqrt(jnp.sqrt(top)) / scale - low
+    tight = jnp.minimum(bound, jnp.maximum(lam, 0.0))
+    gainup = (bound + 2.0 * low) / (tight + 2.0 * low)
+    d0 = 2.0 * low / (tight + 2.0 * low)
+
+    def first(square, d):
         bend = 2.0 / (1.0 + 2.0 * d - d * d)
-        step = jnp.dot(
-            full[...],
-            jnp.concatenate([2.0 * eye - left[:half], -left[half:]], 0),
-            preferred_element_type=jnp.float32,
-            precision=HIGH,
-        )
-        put(bend * step[:half], bend * step[half:])
-        return (4.0 * d - 2.0 * d * d) / (1.0 + 2.0 * d - d * d)
-
-    lax.fori_loop(0, newton_steps(groups * half), newton, d)
-
-    steer = steer_ref[...]
-    w = jnp.dot(full[...], steer, preferred_element_type=jnp.float32, precision=HIGH)
-    for _ in range(REFINE):
-        gap = steer - jnp.dot(mat[...], w, preferred_element_type=jnp.float32, precision=HIGHEST)
-        w = w + jnp.dot(full[...], gap, preferred_element_type=jnp.float32, precision=HIGH)
-    w = w * scale
-    gain = jnp.sum(steer * w, axis=0, keepdims=True)
-    wr = (w[:half] / gain).T
-    wi = (w[half:] / gain).T
-    bins = wr.shape[0]
-    taps_ref[:bins, :half] = wr.astype(jnp.bfloat16)
-    taps_ref[:bins, half:] = wi.astype(jnp.bfloat16)
-    taps_ref[bins:, :half] = (-wi).astype(jnp.bfloat16)
-    taps_ref[bins:, half:] = wr.astype(jnp.bfloat16)
-
-
-def solve(parts, steer, groups):
+        a = acol[...] * gainup
+        eyes = jnp.concatenate([eye, jnp.zeros_like(eye)], 0)
+        xs[...] = bend * (2.0 * eyes - a)
+        ys[...] = bend * (2.0 * a - square * (gainup * gainup))
+        return grow(d)
+
+    def steps_of(d):
+        count = jnp.zeros_like(d)
+        for k in range(2, 12):
+            count = count + jnp.where(d < START[k], 1.0, 0.0)
+        return jnp.max(count).astype(jnp.int32)
+
+    coarse = jnp.max(jnp.where(d0 < COARSE, 1.0, 0.0)) > 0.5
+
+    @pl.when(jnp.logical_not(coarse))
+    def _():
+        d1 = first(square, d0)
+
+        def pack(which):
+            v = xs if which == 0 else ys
+            quads(pair, which * full, v[:half, :].astype(bf16), v[half:, :].astype(bf16))
+
+        pack(0)
+        pack(1)
+
+        def body(_, d):
+            bend = 2.0 / (1.0 + 2.0 * d - d * d)
+            prod = mxu(pair[...], pair[full:, :half])
+            xs[...] = bend * (2.0 * xs[...] - prod[:full])
+            ys[...] = bend * (2.0 * ys[...] - prod[full:])
+            pack(0)
+            pack(1)
+            return grow(d)
+
+        d = lax.fori_loop(0, steps_of(d0), body, d1)
+        bend = 2.0 / (1.0 + 2.0 * d - d * d)
+        xs[...] = bend * (2.0 * xs[...] - mxu(pair[:full, :], pair[full:, :half]))
+        pack(0)
+
+    @pl.when(coarse)
+    def _():
+        quads(low_mat, 0, acol[:half, :], acol[half:, :])
+        exact = jnp.dot(low_mat[...], acol[...], preferred_element_type=f32, precision=HIGH)
+        d1 = first(exact, d0)
+
+        def body(_, d):
+            bend = 2.0 / (1.0 + 2.0 * d - d * d)
+            quads(low_pair, 0, xs[:half, :], xs[half:, :])
+            quads(low_pair, full, ys[:half, :], ys[half:, :])
+            prod = jnp.dot(low_pair[...], ys[...], preferred_element_type=f32, precision=HIGH)
+            xs[...] = bend * (2.0 * xs[...] - prod[:full])
+            ys[...] = bend * (2.0 * ys[...] - prod[full:])
+            return grow(d)
+
+        lax.fori_loop(0, steps_of(d0) + 1, body, d1)
+        quads(pair, 0, xs[:half, :].astype(bf16), xs[half:, :].astype(bf16))
+
+    def refine(w, passes):
+        parts = split(w, passes)
+        gap = mxu(jnp.concatenate(parts, 0), e0[...])
+        if passes == 3:
+            mid = mxu(jnp.concatenate(parts[:2], 0), e1[...])
+            tail = mxu(parts[0], e2[...])
+            fine = (gap[2 * bins:] + mid[bins:] + tail) + (gap[bins:2 * bins] + mid[:bins])
+        else:
+            fine = gap[bins:] + mxu(parts[0], e1[...])
+        rest = (steer[...] - gap[:bins]) - fine
+        return w + mxu(rest.astype(bf16), pair[:full, :]) * gainup
+
+    w = mxu(steer[...].astype(bf16), pair[:full, :]) * gainup
+    w = refine(w, 2)
+    w_ref[...] = refine(w, 2)
+
+    @pl.when(coarse)
+    def _():
+        def body(_, w):
+            return refine(w, 3)
+        w_ref[...] = lax.fori_loop(0, 3, body, w_ref[...])
+
+    w = refine(w_ref[...], 3)
+    gain = jnp.sum(steer[...] * w, axis=1, keepdims=True)
+    w = w / gain
+    wr, wi = w[:, :half], w[:, half:]
+    taps[:bins, :half] = wr.astype(bf16)
+    taps[:bins, half:] = wi.astype(bf16)
+    taps[bins:, :half] = (-wi).astype(bf16)
+    taps[bins:, half:] = wr.astype(bf16)
+
+    for copy in loads:
+        copy.wait()
+    stores = []
+    for k in range(cells // block):
+        span = pl.ds(k * block, block)
+        out_buf[:, span] = lax.dot_general(
+            taps[...], x_buf[span, :], (((1,), (1,)), ((), ())), preferred_element_type=f32
+        ).astype(bf16)
+        copy = pltpu.make_async_copy(out_buf.at[:, span], out_hbm.at[:, span], out_sems.at[k])
+        copy.start()
+        stores.append(copy)
+    for copy in stores:
+        copy.wait()
+
+
+GOAL = 0.95
+START = [start_for(k, GOAL) for k in range(12)]
+COARSE = 0.005
+
+
+def solve(parts, doppler, snaps, groups, block):
     half = parts.shape[2]
-    bins = steer.shape[1]
+    bins = doppler.shape[0]
+    cells, width = snaps.shape
+    full = 2 * half
+    f32, bf16 = jnp.float32, jnp.bfloat16
+    vmem = pltpu.VMEM
+    dma = pltpu.SemaphoreType.DMA
     return pl.pallas_call(
-        functools.partial(solve_kernel, groups),
-        out_shape=jax.ShapeDtypeStruct((2 * bins, 2 * half), jnp.bfloat16),
-        in_specs=[pl.BlockSpec(memory_space=pltpu.VMEM)] * 2,
-        out_specs=pl.BlockSpec(memory_space=pltpu.VMEM),
+        functools.partial(solve_kernel, groups, block),
+        out_shape=jax.ShapeDtypeStruct((2 * bins, cells), bf16),
+        in_specs=[
+            pl.BlockSpec(memory_space=pltpu.VMEM),
+            pl.BlockSpec(memory_space=pltpu.VMEM),
+            pl.BlockSpec(memory_space=pl.ANY),
+        ],
+        out_specs=pl.BlockSpec(memory_space=pl.ANY),
         scratch_shapes=[
-            pltpu.VMEM((2 * half, 2 * half), jnp.float32),
-            pltpu.VMEM((2 * half, 2 * half), jnp.float32),
-            pltpu.VMEM((2 * half, half), jnp.float32),
+            vmem((cells, width), bf16),
+            vmem((2 * bins, cells), bf16),
+            vmem((2 * bins, width), bf16),
+            vmem((full, full), bf16),
+            vmem((full, full), bf16),
+            vmem((full, full), bf16),
+            vmem((full, full), f32),
+            vmem((2 * full, full), f32),
+            vmem((2 * full, full), bf16),
+            vmem((full, half), f32),
+            vmem((full, half), f32),
+            vmem((full, half), f32),
+            vmem((bins, full), f32),
+            vmem((bins, full), f32),
+            dma((cells // block,)),
+            dma((cells // block,)),
         ],
         name="solve",
-    )(parts, steer)
-
-
-def filter_kernel(taps_ref, x_ref, out_ref):
-    out_ref[...] = lax.dot_general(
-        taps_ref[...], x_ref[...], (((1,), (1,)), ((), ())), preferred_element_type=jnp.float32
-    ).astype(out_ref.dtype)
-
-
-def apply_taps(taps, snaps, block):
-    cells, width = snaps.shape
-    rows = taps.shape[0]
-    return pl.pallas_call(
-        filter_kernel,
-        grid=(cells // block,),
-        in_specs=[
-            pl.BlockSpec((rows, width), lambda i: (0, 0)),
-            pl.BlockSpec((block, width), lambda i: (i, 0)),
-        ],
-        out_specs=pl.BlockSpec((rows, block), lambda i: (0, i)),
-        out_shape=jax.ShapeDtypeStruct((rows, cells), jnp.bfloat16),
-        name="filter",
-    )(taps, snaps)
+    )(parts, doppler, snaps)
 
 
 def per_device(snapshots, training, doppler):
@@ -307,9 +446,7 @@
     block = min(4096, snaps.shape[0])
     packed = gram(snaps, training[None, :], block)
     parts = all_sum(packed)
-    steer = steering(doppler[0], CHANNELS, PULSES)
-    taps = solve(parts, steer, lax.axis_size("bins"))
-    return apply_taps(taps, snaps, block)[None]
+    return solve(parts, doppler[0][:, None], snaps, lax.axis_size("bins"), 1024)[None]
 
 
 def solution(mesh):

time: 54.7 us -> 37.8 us (0.69); the launches traced: 53.8 us -> 37.7 us
  Pallas kernels: 51.9 us -> 36.3 us
  other arithmetic: 1.97 us -> 0 us
  local copies, waits for them, and re-layouts: 0 us -> 1.39 us
    pallas_call x2 -> x1, Pallas kernels: 25 us -> 9.38 us  [solve(): pl.pallas_call(functools.partial(solve_kernel, groups, block), out_shape=...]
    another operation x0 -> x1, local copies, waits for them, and re-layouts: none -> 1.39 us  [per_device(): doppler[0][:, None]]
    div x1 -> x0, other arithmetic: 0.72 us -> none  [steering(): jnp.concatenate([jnp.cos(phase), jnp.sin(phase)], 0)]
    mul x2 -> x0, other arithmetic: 0.66 us -> none  [the longest x1 0.66 us: steering(): pulse[:, None] * freq[None, :]]
    cos x1 -> x0, other arithmetic: 0.58 us -> none  [steering(): jnp.cos(phase)]
where the time goes in v1:
time: 37.8 us; the launch traced here: 37.7 us
  Pallas kernels  36.3 us (96%)
  local copies, waits for them, and re-layouts  1.39 us (4%)
    pallas_call x1, Pallas kernels, all_sum(): pl.pallas_call(functools.partial(sum_kernel, n, m), out_shape=jax.ShapeDt...  20.1 us
    pallas_call x1, Pallas kernels, solve(): pl.pallas_call(functools.partial(solve_kernel, groups, block), out_shape=...  9.38 us
    pallas_call x1, Pallas kernels, gram(): pl.pallas_call(functools.partial(gram_kernel, half), grid=(cells // block...  6.75 us
    another operation x1, local copies, waits for them, and re-layouts, per_device(): doppler[0][:, None]  1.39 us

profile of v1, /device:TPU:0, one launch (start us, length us, event | category | flops | bytes accessed | tf_op | source)
XLA Modules:
  0.0 37.7 jit_solution(15056258411214361716)
XLA Ops:
  0.0 1.4 %copy.4.dop_ref = s32[128,1]{1,0:T(8,128)} copy(s32[128,1]{0,1:T(1,128)} %bitcast.7) | data formatting | bytes 1024 | tf_op jit(solution)/shard_map/broadcast_in_dim;squeeze | solution.py:449
  1.4 6.8 %gram.1.x_ref = f32[256,256]{1,0:T(8,128)} custom-call(bf16[8192,512]{1,0:T(8,128)(2,1)} %bitcast.4, s32[1,8192]{1,0:T(1,128)} %bitcast.6), custom_call_target="tpu_custom_call" | custom-call | tf_op jit(solution)/shard_map/gram/pallas_call | solution.py:56
  8.1 20.1 %all_sum.1.parts_ref = f32[8,40,256]{2,1,0:T(8,128)} custom-call(f32[256,256]{1,0:T(8,128)} %gram.1.x_ref), custom_call_target="tpu_custom_call" | custom-call | tf_op jit(solution)/shard_map/all_sum/pallas_call | solution.py:160
  28.3 9.4 %solve.1 = bf16[256,8192]{1,0:T(8,128)(2,1)} custom-call(f32[8,40,256]{2,1,0:T(8,128)} %all_sum.1.parts_ref, s32[128,1]{1,0:T(8,128)} %copy.4.dop_ref, bf16[8192,512]{1,0:T(8,128)(2,1)} %bitcast.5), custom_call_target="tpu_custom_call" | custom-call | tf_op jit(solution)/shard_map/solve/pallas_call | solution.py:413

commit v2 on v1

v2 whole, which is shorter than its diff:
```python
import functools
import math

import jax
import jax.numpy as jnp
from jax import lax
from jax.experimental import pallas as pl
from jax.experimental.pallas import tpu as pltpu
from jax.sharding import PartitionSpec as P

CHANNELS = 16
PULSES = 16
NDOPP = 1024


load_ratio = 0.5
look_freq = 0.125

EXTRA = 8
HIGH = lax.Precision.HIGH
MESH = pl.DeviceIdType.MESH


def sum_kernel(
    n, m, chunks, blocks, keep_hbm, x_hbm, out_ref,
    keep_ref, x_buf, acc, cross, packed, rs_buf, tr_src, tr_buf, mine, keep_sem, in_sems, sems,
):
    me = lax.axis_index("cells")
    g = lax.axis_index("bins")
    cells, width = x_buf.shape
    half = width // 2
    side = half // 2
    rows = half // (n * chunks)
    rs_send, rs_recv, tr_send, tr_recv, ag_send, ag_recv = sems
    block = cells // blocks

    for k in range(blocks):
        span = pl.ds(k * block, block)
        copy = pltpu.make_async_copy(x_hbm.at[span], x_buf.at[span], in_sems.at[k])
        copy.start()

    keep_copy = pltpu.make_async_copy(keep_hbm, keep_ref, keep_sem)
    keep_copy.start()
    barrier = pltpu.get_barrier_semaphore()
    for k in range(1, n):
        pl.semaphore_signal(
            barrier, inc=1, device_id=(lax.rem(me + k, n), g), device_id_type=MESH
        )
    for k in range(1, m):
        pl.semaphore_signal(
            barrier, inc=1, device_id=(me, lax.rem(g + k, m)), device_id_type=MESH
        )

    r = lax.broadcasted_iota(jnp.int32, (side, side), 0)
    c = lax.broadcasted_iota(jnp.int32, (side, side), 1)

    def products(part, k):
        span = pl.ds(pl.multiple_of(k * block, block), block)
        keep = keep_ref[:, span].astype(jnp.bfloat16)
        mr = x_buf[span, part * side:(part + 1) * side].T * keep
        mi = x_buf[span, half + part * side:half + (part + 1) * side].T * keep
        both = jnp.dot(
            jnp.concatenate([mr, mi], 0), x_buf[span, half:], preferred_element_type=jnp.float32
        )
        real = jnp.dot(mr, x_buf[span, :half], preferred_element_type=jnp.float32)
        acc[:half, :] += both
        acc[half:, :] += real

    def send(k):
        for j in range(1, n):
            peer = lax.rem(me + j, n)
            copy = pltpu.make_async_remote_copy(
                src_ref=packed.at[pl.ds(pl.multiple_of((k * n + peer) * rows, rows), rows)],
                dst_ref=rs_buf.at[k, j - 1],
                send_sem=rs_send.at[k, j - 1],
                recv_sem=rs_recv.at[k, j - 1],
                device_id=(peer, g),
                device_id_type=MESH,
            )
            copy.start()
            scatters.append(copy)

    scatters = []
    keep_copy.wait()

    def fresh(k, _):
        span = pl.ds(pl.multiple_of(k * block, block), block)
        pltpu.make_async_copy(x_hbm.at[span], x_buf.at[span], in_sems.at[k]).wait()
        products(0, k)
        return 0

    acc[...] = jnp.zeros_like(acc)
    lax.fori_loop(0, blocks, fresh, 0)
    cr = acc[:side, :]
    re = acc[side:half, :] + acc[half:, :]
    cross[...] = cr[:, side:]
    packed[:side, :side] = jnp.where(r <= c, re[:, :side], cr[:, :side].T - cr[:, :side])
    packed[:side, side:] = re[:, side:]
    trace = jnp.sum(jnp.where(r == c, re[:, :side], 0.0), axis=0, keepdims=True)
    pl.semaphore_wait(barrier, n + m - 2)
    early = chunks // 2
    for k in range(early):
        send(k)

    def again(k, _):
        products(1, k)
        return 0

    acc[...] = jnp.zeros_like(acc)
    lax.fori_loop(0, blocks, again, 0)
    cr = acc[:side, :]
    re = acc[side:half, side:] + acc[half:, side:]
    packed[side:, :side] = cross[...].T - cr[:, :side]
    packed[side:, side:] = jnp.where(r <= c, re, cr[:, side:].T - cr[:, side:])
    trace = trace + jnp.sum(jnp.where(r == c, re, 0.0), axis=0, keepdims=True)
    tr_src[...] = jnp.broadcast_to(trace, tr_src.shape)
    traces = []
    for k in range(1, m):
        copy = pltpu.make_async_remote_copy(
            src_ref=tr_src,
            dst_ref=tr_buf.at[k - 1],
            send_sem=tr_send.at[k - 1],
            recv_sem=tr_recv.at[k - 1],
            device_id=(me, lax.rem(g + k, m)),
            device_id_type=MESH,
        )
        copy.start()
        traces.append(copy)
    for k in range(early, chunks):
        send(k)

    gathers = []
    for k in range(chunks):
        for copy in scatters[k * (n - 1):(k + 1) * (n - 1)]:
            copy.wait()
        total = packed[pl.ds(pl.multiple_of((k * n + me) * rows, rows), rows), :]
        for j in range(n - 1):
            total = total + rs_buf[k, j]
        mine[k, :rows, :] = total
        out_ref[k, me, :rows, :] = total
        size = rows
        if k == chunks - 1:
            for copy in traces:
                copy.wait()
            power = tr_src[...]
            for j in range(m - 1):
                power = power + tr_buf[j]
            mine[k, rows:, :side] = power
            out_ref[k, me, rows:, :side] = power
            mine[k, rows:, side:] = jnp.zeros_like(power)
            size = rows + EXTRA
        for j in range(1, n):
            copy = pltpu.make_async_remote_copy(
                src_ref=mine.at[k, pl.ds(0, size)],
                dst_ref=out_ref.at[k, me, pl.ds(0, size)],
                send_sem=ag_send.at[k, j - 1],
                recv_sem=ag_recv.at[k, j - 1],
                device_id=(lax.rem(me + j, n), g),
                device_id_type=MESH,
            )
            copy.start()
            gathers.append((k, j, size, copy))
    for k, j, size, copy in gathers:
        copy.wait_send()
        peer = lax.rem(me + n - j, n)
        pltpu.make_async_remote_copy(
            src_ref=mine.at[k, pl.ds(0, size)],
            dst_ref=out_ref.at[k, peer, pl.ds(0, size)],
            send_sem=ag_send.at[k, j - 1],
            recv_sem=ag_recv.at[k, j - 1],
            device_id=(peer, g),
            device_id_type=MESH,
        ).wait_recv()


def gram_sum(snaps, keep):
    n, m = lax.axis_size("cells"), lax.axis_size("bins")
    cells, width = snaps.shape
    half = width // 2
    side = half // 2
    chunks = max(1, min(CHUNKS, half // (8 * n)))
    rows = half // (n * chunks)
    blocks = max(1, cells // 1024)
    dma = pltpu.SemaphoreType.DMA
    f32, vmem = jnp.float32, pltpu.VMEM
    return pl.pallas_call(
        functools.partial(sum_kernel, n, m, chunks, blocks),
        out_shape=jax.ShapeDtypeStruct((chunks, n, rows + EXTRA, half), f32),
        in_specs=[pl.BlockSpec(memory_space=pltpu.HBM)] * 2,
        out_specs=pl.BlockSpec(memory_space=pltpu.VMEM),
        scratch_shapes=[
            vmem((1, cells), jnp.int32),
            vmem((cells, width), jnp.bfloat16),
            vmem((half + side, half), f32),
            vmem((side, side), f32),
            vmem((half, half), f32),
            vmem((chunks, n - 1, rows, half), f32),
            vmem((EXTRA, side), f32),
            vmem((m - 1, EXTRA, side), f32),
            vmem((chunks, rows + EXTRA, half), f32),
            dma(()),
            dma((blocks,)),
            [dma((chunks, n - 1)), dma((chunks, n - 1)), dma((m - 1,)), dma((m - 1,)), dma((chunks, n - 1)), dma((chunks, n - 1))],
        ],
        compiler_params=pltpu.CompilerParams(
            collective_id=0, has_side_effects=True, vmem_limit_bytes=VMEM_LIMIT
        ),
        name="gram_sum",
    )(keep, snaps)


def grow(d):
    return (4.0 * d - 2.0 * d * d) / (1.0 + 2.0 * d - d * d)


def start_for(steps, goal):
    lo, hi = 0.0, 1.0
    for _ in range(100):
        mid = 0.5 * (lo + hi)
        d = mid
        for _ in range(steps):
            d = grow(d)
        lo, hi = (lo, mid) if d >= goal else (mid, hi)
    return hi


def split(x, parts):
    out = []
    for _ in range(parts):
        top = x.astype(jnp.bfloat16)
        out.append(top)
        x = x - top.astype(jnp.float32)
    return out


def mxu(a, b):
    return jnp.dot(a, b, preferred_element_type=jnp.float32)


def total(x):
    return jnp.sum(jnp.sum(x, axis=0, keepdims=True), axis=1, keepdims=True)


def steer_rows(doppler, chans, pulses):
    bins, dim = doppler.shape[1], chans * pulses
    at = lax.broadcasted_iota(jnp.int32, (bins, bins), 0)
    to = lax.broadcasted_iota(jnp.int32, (bins, bins), 1)
    doppler = jnp.sum(
        jnp.where(at == to, doppler.astype(jnp.float32), 0.0), axis=1, keepdims=True
    )
    index = lax.broadcasted_iota(jnp.int32, (1, dim), 1)
    pulse = lax.rem(index, pulses)
    chan = ((index - pulse) // pulses).astype(jnp.float32)
    freq = doppler * (1.0 / NDOPP) - 0.5
    turns = look_freq * chan + pulse.astype(jnp.float32) * freq
    phase = (2.0 * math.pi) * turns
    quarter = jnp.floor(4.0 * turns + 0.5)
    rest = phase - quarter * 1.5703125
    rest = rest - quarter * 4.837512969970703125e-4
    rest = rest - quarter * 7.549789948768648e-8
    sq = rest * rest
    sin = rest + rest * sq * (
        -1.6666654611e-1 + sq * (8.3321608736e-3 + sq * -1.9515295891e-4)
    )
    cos = 1.0 + sq * (
        -0.5 + sq * (4.166664568298827e-2 + sq * (-1.388731625493765e-3 + sq * 2.443315711809948e-5))
    )
    which = quarter.astype(jnp.int32) & 3
    odd = (which & 1) == 1
    c = jnp.where(odd, sin, cos)
    s = jnp.where(odd, cos, sin)
    c = jnp.where((which == 1) | (which == 2), -c, c)
    s = jnp.where(which >= 2, -s, s)
    return jnp.concatenate([c, s], 1) * (1.0 / math.sqrt(dim))


def solve_kernel(
    groups, block, parts_ref, dop_hbm, x_hbm, out_hbm,
    dop, x_buf, out_buf, taps, re_parts, im_parts, pair, wide, xs, ys, acol, steer, w_ref,
    dop_sem, in_sems, out_sems,
):
    chunks, n = parts_ref.shape[:2]
    rows = parts_ref.shape[2] - EXTRA
    half = parts_ref.shape[3]
    full = 2 * half
    bins = dop.shape[1]
    cells = x_buf.shape[0]
    f32, bf16 = jnp.float32, jnp.bfloat16

    dop_copy = pltpu.make_async_copy(dop_hbm, dop, dop_sem)
    dop_copy.start()
    loads = []
    for k in range(cells // block):
        span = pl.ds(k * block, block)
        copy = pltpu.make_async_copy(x_hbm.at[span], x_buf.at[span], in_sems.at[k])
        copy.start()
        loads.append(copy)

    summed = jnp.concatenate(
        [parts_ref[k, j, :rows, :] for k in range(chunks) for j in range(n)], 0
    )
    power_row = parts_ref[chunks - 1, 0, rows:rows + 1, :half // 2]
    for k in range(1, n):
        power_row = power_row + parts_ref[chunks - 1, k, rows:rows + 1, :half // 2]
    noise = jnp.sum(power_row, axis=1, keepdims=True) / (groups * half)
    low = load_ratio * noise
    r = lax.broadcasted_iota(jnp.int32, (half, half), 0)
    c = lax.broadcasted_iota(jnp.int32, (half, half), 1)
    trace = total(jnp.where(r == c, summed, 0.0))
    unit = 1.0 / (trace + low)
    norm = summed * unit
    norm = norm * norm
    fro = jnp.sqrt(total(jnp.where(r == c, norm, norm + norm))) * (trace + low)
    bound = jnp.minimum(trace, 1.0001 * fro)
    scale = 2.0 / (bound + 2.0 * low)
    eye = jnp.where(r == c, 1.0, 0.0)
    flip = summed.T
    real = (jnp.where(r <= c, summed, flip) + low * eye) * scale
    imag = jnp.where(r > c, summed, jnp.where(r < c, -flip, 0.0)) * scale
    acol[:half, :] = real
    acol[half:, :] = imag
    for k, (xr, xi) in enumerate(zip(split(real, 3), split(imag, 3))):
        re_parts[k * half:(k + 1) * half, :] = xr
        im_parts[k * half:(k + 1) * half, :] = xi
        if k == 0:
            pair[:half, :] = xr
            pair[half:full, :] = xi

    def times(left, re, im):
        rows = left.shape[0] // 2
        p, q = mxu(left, re), mxu(left, im)
        return p[:rows] - q[rows:], p[rows:] + q[:rows]

    square = jnp.concatenate(times(pair[:full, :], re_parts[:half, :], im_parts[:half, :]), 0)
    top = total(square * square)
    dop_copy.wait()
    steer[...] = steer_rows(dop[...], CHANNELS, PULSES)

    lam = 1.005 * jnp.sqrt(jnp.sqrt(top)) / scale - low
    tight = jnp.minimum(bound, jnp.maximum(lam, 0.0))
    gainup = (bound + 2.0 * low) / (tight + 2.0 * low)
    d0 = 2.0 * low / (tight + 2.0 * low)

    def bend_of(d):
        return 2.0 / (1.0 + 2.0 * d - d * d)

    def pack(at, v):
        pair[at * half:at * half + full, :] = v.astype(bf16)

    def first(square, d):
        bend = bend_of(d)
        a = acol[...] * (bend * gainup)
        x1 = -a
        xs[...] = jnp.concatenate([x1[:half] + (2.0 * bend) * eye, x1[half:]], 0)
        ys[...] = 2.0 * a - square * (bend * gainup * gainup)
        return grow(d)

    def steps_of(d):
        count = jnp.zeros_like(d)
        for k in range(2, 12):
            count = count + jnp.where(d < START[k], 1.0, 0.0)
        return jnp.max(count).astype(jnp.int32)

    coarse = jnp.max(jnp.where(d0 < COARSE, 1.0, 0.0)) > 0.5

    @pl.when(jnp.logical_not(coarse))
    def _():
        d1 = first(square, d0)
        pack(0, xs[...])
        pack(2, ys[...])

        def body(_, d):
            bend = bend_of(d)
            p = mxu(pair[...], pair[full:full + half, :])
            q = mxu(pair[...], pair[full + half:, :])
            for at, ref in ((0, xs), (full, ys)):
                re = bend * (2.0 * ref[:half, :] - (p[at:at + half] - q[at + half:at + full]))
                im = bend * (2.0 * ref[half:, :] - (p[at + half:at + full] + q[at:at + half]))
                ref[:half, :] = re
                ref[half:, :] = im
                pair[at:at + half, :] = re.astype(bf16)
                pair[at + half:at + full, :] = im.astype(bf16)
            return grow(d)

        d = lax.fori_loop(0, steps_of(d0), body, d1)
        bend = bend_of(d)
        re, im = times(pair[:full, :], pair[full:full + half, :], pair[full + half:, :])
        pair[:half, :] = (bend * (2.0 * xs[:half, :] - re)).astype(bf16)
        pair[half:full, :] = (bend * (2.0 * xs[half:, :] - im)).astype(bf16)

    @pl.when(coarse)
    def _():
        def product(left, ref):
            wide[:half, :half] = left[:half]
            wide[half:, half:] = left[:half]
            wide[:half, half:] = -left[half:]
            wide[half:, :half] = left[half:]
            return jnp.dot(wide[...], ref[...], preferred_element_type=f32, precision=HIGH)

        d1 = first(product(acol[...], acol), d0)

        def body(_, d):
            bend = bend_of(d)
            xs[...] = bend * (2.0 * xs[...] - product(xs[...], ys))
            ys[...] = bend * (2.0 * ys[...] - product(ys[...], ys))
            return grow(d)

        lax.fori_loop(0, steps_of(d0) + 1, body, d1)
        pack(0, xs[...])

    def stack(v):
        return jnp.concatenate([v[:, :half], v[:, half:]], 0).astype(bf16)

    def apply(v):
        left = stack(v)
        p, q = mxu(left, pair[:half, :]), mxu(left, pair[half:full, :])
        return jnp.concatenate([p[:bins] + q[bins:], p[bins:] - q[:bins]], 1) * gainup

    def short(v):
        return v.astype(bf16).astype(f32)

    def less(rest, w, parts):
        left = jnp.concatenate([stack(w)] * parts, 1)
        p = mxu(left, re_parts[:parts * half, :])
        q = mxu(left, im_parts[:parts * half, :])
        return rest - jnp.concatenate([p[:bins] + q[bins:], p[bins:] - q[:bins]], 1)

    w0 = short(apply(steer[...]))
    rest = less(steer[...], w0, 3)
    w1 = short(apply(rest))
    rest = less(rest, w1, 3)
    w2 = short(apply(rest))
    rest = less(rest, w2, 2)
    w_ref[...] = w0 + (w1 + (w2 + apply(rest)))

    @pl.when(coarse)
    def _():
        def body(_, w):
            rest = steer[...]
            for part in split(w, 3):
                rest = less(rest, part.astype(f32), 3)
            return w + apply(rest)
        w_ref[...] = lax.fori_loop(0, 4, body, w_ref[...])

    w = w_ref[...]
    gain = jnp.sum(steer[...] * w, axis=1, keepdims=True)
    w = w / gain
    wr, wi = w[:, :half], w[:, half:]
    taps[:bins, :half] = wr.astype(bf16)
    taps[:bins, half:] = wi.astype(bf16)
    taps[bins:, :half] = (-wi).astype(bf16)
    taps[bins:, half:] = wr.astype(bf16)

    for copy in loads:
        copy.wait()
    stores = []
    for k in range(cells // block):
        span = pl.ds(k * block, block)
        out_buf[:, span] = lax.dot_general(
            taps[...], x_buf[span, :], (((1,), (1,)), ((), ())), preferred_element_type=f32
        ).astype(bf16)
        copy = pltpu.make_async_copy(out_buf.at[:, span], out_hbm.at[:, span], out_sems.at[k])
        copy.start()
        stores.append(copy)
    for copy in stores:
        copy.wait()


GOAL = 0.95
START = [start_for(k, GOAL) for k in range(12)]
COARSE = 0.005
CHUNKS = 2
VMEM_LIMIT = 52 * 1024 * 1024


def solve(parts, doppler, snaps, groups, block):
    half = parts.shape[3]
    bins = doppler.shape[1]
    cells, width = snaps.shape
    full = 2 * half
    f32, bf16 = jnp.float32, jnp.bfloat16
    vmem = pltpu.VMEM
    dma = pltpu.SemaphoreType.DMA
    return pl.pallas_call(
        functools.partial(solve_kernel, groups, block),
        out_shape=jax.ShapeDtypeStruct((2 * bins, cells), bf16),
        in_specs=[
            pl.BlockSpec(memory_space=pltpu.VMEM),
            pl.BlockSpec(memory_space=pltpu.HBM),
            pl.BlockSpec(memory_space=pltpu.HBM),
        ],
        out_specs=pl.BlockSpec(memory_space=pltpu.HBM),
        scratch_shapes=[
            vmem((1, bins), jnp.int32),
            vmem((cells, width), bf16),
            vmem((2 * bins, cells), bf16),
            vmem((2 * bins, width), bf16),
            vmem((3 * half, half), bf16),
            vmem((3 * half, half), bf16),
            vmem((2 * full, half), bf16),
            vmem((full, full), f32),
            vmem((full, half), f32),
            vmem((full, half), f32),
            vmem((full, half), f32),
            vmem((bins, full), f32),
            vmem((bins, full), f32),
            dma(()),
            dma((cells // block,)),
            dma((cells // block,)),
        ],
        compiler_params=pltpu.CompilerParams(vmem_limit_bytes=VMEM_LIMIT),
        name="solve",
    )(parts, doppler, snaps)


def per_device(snapshots, training, doppler):
    snaps = snapshots[0]
    parts = gram_sum(snaps, training[None, :])
    return solve(parts, doppler, snaps, lax.axis_size("bins"), 1024)[None]


def solution(mesh):
    in_specs = (P("bins", "cells", None), P("cells"), P("bins", None))
    out_specs = P("bins", None, "cells")
    return jax.shard_map(
        per_device, mesh=mesh, in_specs=in_specs, out_specs=out_specs, check_vma=False
    )
```

time: 37.8 us -> 33 us (0.87); the launches traced: 37.7 us -> 32.3 us
  Pallas kernels: 36.3 us -> 31.5 us
  local copies, waits for them, and re-layouts: 1.39 us -> 0.77 us
    pallas_call x2 -> x1, Pallas kernels: 26.9 us -> 23.5 us  [gram_sum(): pl.pallas_call(functools.partial(sum_kernel, n, m, chunks, blocks), out_s...]
    pallas_call x1, Pallas kernels: 9.38 us -> 7.98 us  [solve(): pl.pallas_call(functools.partial(solve_kernel, groups, block), out_shape=...]
    another operation x1 -> x0, local copies, waits for them, and re-layouts: 1.39 us -> none  [per_device(): doppler[0][:, None]]
    unnamed x0 -> x4, local copies, waits for them, and re-layouts: none -> 0.77 us
where the time goes in v2:
time: 33 us; the launch traced here: 32.3 us
  Pallas kernels  31.5 us (95%)
  local copies, waits for them, and re-layouts  0.77 us (2%)
    pallas_call x1, Pallas kernels, gram_sum(): pl.pallas_call(functools.partial(sum_kernel, n, m, chunks, blocks), out_s...  23.5 us
    pallas_call x1, Pallas kernels, solve(): pl.pallas_call(functools.partial(solve_kernel, groups, block), out_shape=...  7.98 us
    unnamed x4, local copies, waits for them, and re-layouts  0.77 us

profile of v2, /device:TPU:0, one launch (start us, length us, event | category | flops | bytes accessed | tf_op | source)
XLA Modules:
  0.0 32.3 jit_solution(13051157937888227147)
XLA Ops:
  0.0 0.0 copy-start.1
  0.0 0.0 copy-start
  0.0 0.8 %copy-done = s32[8192]{0:T(1024)S(1)} copy-done((s32[8192]{0:T(1024)S(1)}, s32[8192]{0:T(1024)}, u32[]{:S(2)}) %copy-start) | copy-done | bytes 32792
  0.8 23.5 %gram_sum.1.parts_ref = f32[2,8,24,256]{3,2,1,0:T(8,128)S(1)} custom-call(s32[1,8192]{1,0:T(1,128)S(1)} %bitcast.3, bf16[8192,512]{1,0:T(8,128)(2,1)} %bitcast.4), custom_call_target="tpu_custom_call" | custom-call | tf_op jit(solution)/shard_map/gram_sum/pallas_call | solution.py:186
  24.3 0.0 copy-done.1
  24.3 8.0 %solve.1 = bf16[256,8192]{1,0:T(8,128)(2,1)} custom-call(f32[2,8,24,256]{3,2,1,0:T(8,128)S(1)} %gram_sum.1.parts_ref, s32[1,128]{1,0:T(1,128)S(1)} %copy-done.1, bf16[8192,512]{1,0:T(8,128)(2,1)} %bitcast.5), custom_call_target="tpu_custom_call" | custom-call | tf_op jit(solution)/shard_map/solve/pallas_call | solution.py:484
Async XLA Ops:
  0.0 24.3 %copy-start.1 = (s32[1,128]{1,0:T(1,128)S(1)}, s32[1,128]{1,0:T(1,128)}, u32[]{:S(2)}) copy-start(s32[1,128]{1,0:T(1,128)} %dop_hbm.1) | copy-start | bytes 1540
  0.0 0.8 %copy-start = (s32[8192]{0:T(1024)S(1)}, s32[8192]{0:T(1024)}, u32[]{:S(2)}) copy-start(s32[8192]{0:T(1024)} %param.4) | copy-start | bytes 98308

commit v3 on v2

--- a/solution.py
+++ b/solution.py
@@ -16,14 +16,13 @@
 load_ratio = 0.5
 look_freq = 0.125
 
-EXTRA = 8
 HIGH = lax.Precision.HIGH
 MESH = pl.DeviceIdType.MESH
 
 
 def sum_kernel(
-    n, m, chunks, blocks, keep_hbm, x_hbm, out_ref,
-    keep_ref, x_buf, acc, cross, packed, rs_buf, tr_src, tr_buf, mine, keep_sem, in_sems, sems,
+    n, m, chunks, blocks, keep_hbm, x_hbm, out_ref, pw_ref,
+    keep_ref, x_buf, acc, late, cross, packed, rs_buf, tr_src, tr_buf, pw_src, mine, keep_sem, in_sems, sems,
 ):
     me = lax.axis_index("cells")
     g = lax.axis_index("bins")
@@ -31,14 +30,12 @@
     half = width // 2
     side = half // 2
     rows = half // (n * chunks)
-    rs_send, rs_recv, tr_send, tr_recv, ag_send, ag_recv = sems
+    rs_send, rs_recv, tr_send, tr_recv, pw_send, pw_recv, ag_send, ag_recv = sems
     block = cells // blocks
 
-    for k in range(blocks):
+    for k in range(min(DEPTH, blocks)):
         span = pl.ds(k * block, block)
-        copy = pltpu.make_async_copy(x_hbm.at[span], x_buf.at[span], in_sems.at[k])
-        copy.start()
-
+        pltpu.make_async_copy(x_hbm.at[span], x_buf.at[span], in_sems.at[k]).start()
     keep_copy = pltpu.make_async_copy(keep_hbm, keep_ref, keep_sem)
     keep_copy.start()
     barrier = pltpu.get_barrier_semaphore()
@@ -54,17 +51,12 @@
     r = lax.broadcasted_iota(jnp.int32, (side, side), 0)
     c = lax.broadcasted_iota(jnp.int32, (side, side), 1)
 
-    def products(part, k):
+    def turned(span, at):
+        return x_buf[span, at:at + side].T * keep_ref[:, span].astype(jnp.bfloat16)
+
+    def load(k):
         span = pl.ds(pl.multiple_of(k * block, block), block)
-        keep = keep_ref[:, span].astype(jnp.bfloat16)
-        mr = x_buf[span, part * side:(part + 1) * side].T * keep
-        mi = x_buf[span, half + part * side:half + (part + 1) * side].T * keep
-        both = jnp.dot(
-            jnp.concatenate([mr, mi], 0), x_buf[span, half:], preferred_element_type=jnp.float32
-        )
-        real = jnp.dot(mr, x_buf[span, :half], preferred_element_type=jnp.float32)
-        acc[:half, :] += both
-        acc[half:, :] += real
+        return pltpu.make_async_copy(x_hbm.at[span], x_buf.at[span], in_sems.at[k])
 
     def send(k):
         for j in range(1, n):
@@ -84,15 +76,24 @@
     keep_copy.wait()
 
     def fresh(k, _):
+        load(k).wait()
+
+        @pl.when(k + DEPTH < blocks)
+        def _():
+            load(k + DEPTH).start()
+
         span = pl.ds(pl.multiple_of(k * block, block), block)
-        pltpu.make_async_copy(x_hbm.at[span], x_buf.at[span], in_sems.at[k]).wait()
-        products(0, k)
+        mr = turned(span, 0)
+        left = jnp.concatenate([mr, turned(span, half), turned(span, half + side)], 0)
+        acc[:3 * side, :] += jnp.dot(left, x_buf[span, half:], preferred_element_type=jnp.float32)
+        acc[3 * side:, :] += jnp.dot(mr, x_buf[span, :half], preferred_element_type=jnp.float32)
         return 0
 
     acc[...] = jnp.zeros_like(acc)
+    late[...] = jnp.zeros_like(late)
     lax.fori_loop(0, blocks, fresh, 0)
     cr = acc[:side, :]
-    re = acc[side:half, :] + acc[half:, :]
+    re = acc[side:half, :] + acc[3 * side:, :]
     cross[...] = cr[:, side:]
     packed[:side, :side] = jnp.where(r <= c, re[:, :side], cr[:, :side].T - cr[:, :side])
     packed[:side, side:] = re[:, side:]
@@ -103,17 +104,18 @@
         send(k)
 
     def again(k, _):
-        products(1, k)
+        span = pl.ds(pl.multiple_of(k * wide, wide), wide)
+        late[...] += jnp.dot(turned(span, side), x_buf[span, :], preferred_element_type=jnp.float32)
         return 0
 
-    acc[...] = jnp.zeros_like(acc)
-    lax.fori_loop(0, blocks, again, 0)
-    cr = acc[:side, :]
-    re = acc[side:half, side:] + acc[half:, side:]
+    wide = min(WIDE, cells)
+    lax.fori_loop(0, cells // wide, again, 0)
+    cr = late[:, half:]
+    re = acc[half:half + side, side:] + late[:, side:half]
     packed[side:, :side] = cross[...].T - cr[:, :side]
     packed[side:, side:] = jnp.where(r <= c, re, cr[:, side:].T - cr[:, side:])
     trace = trace + jnp.sum(jnp.where(r == c, re, 0.0), axis=0, keepdims=True)
-    tr_src[...] = jnp.broadcast_to(trace, tr_src.shape)
+    tr_src[...] = trace
     traces = []
     for k in range(1, m):
         copy = pltpu.make_async_remote_copy(
@@ -131,41 +133,62 @@
 
     gathers = []
     for k in range(chunks):
-        for copy in scatters[k * (n - 1):(k + 1) * (n - 1)]:
-            copy.wait()
-        total = packed[pl.ds(pl.multiple_of((k * n + me) * rows, rows), rows), :]
-        for j in range(n - 1):
-            total = total + rs_buf[k, j]
-        mine[k, :rows, :] = total
-        out_ref[k, me, :rows, :] = total
-        size = rows
         if k == chunks - 1:
             for copy in traces:
                 copy.wait()
             power = tr_src[...]
             for j in range(m - 1):
                 power = power + tr_buf[j]
-            mine[k, rows:, :side] = power
-            out_ref[k, me, rows:, :side] = power
-            mine[k, rows:, side:] = jnp.zeros_like(power)
-            size = rows + EXTRA
+            both = jnp.concatenate([power, tr_src[...]], 0)
+            pw_src[...] = both
+            pw_ref[me] = both
+            spread = []
+            for j in range(1, n):
+                copy = pltpu.make_async_remote_copy(
+                    src_ref=pw_src,
+                    dst_ref=pw_ref.at[me],
+                    send_sem=pw_send.at[j - 1],
+                    recv_sem=pw_recv.at[j - 1],
+                    device_id=(lax.rem(me + j, n), g),
+                    device_id_type=MESH,
+                )
+                copy.start()
+                spread.append(copy)
+        for copy in scatters[k * (n - 1):(k + 1) * (n - 1)]:
+            copy.wait()
+        total = packed[pl.ds(pl.multiple_of((k * n + me) * rows, rows), rows), :]
+        for j in range(n - 1):
+            total = total + rs_buf[k, j]
+        mine[k] = total
+        out_ref[k, me] = total
         for j in range(1, n):
             copy = pltpu.make_async_remote_copy(
-                src_ref=mine.at[k, pl.ds(0, size)],
-                dst_ref=out_ref.at[k, me, pl.ds(0, size)],
+                src_ref=mine.at[k],
+                dst_ref=out_ref.at[k, me],
                 send_sem=ag_send.at[k, j - 1],
                 recv_sem=ag_recv.at[k, j - 1],
                 device_id=(lax.rem(me + j, n), g),
                 device_id_type=MESH,
             )
             copy.start()
-            gathers.append((k, j, size, copy))
-    for k, j, size, copy in gathers:
+            gathers.append((k, j, copy))
+    for j in range(1, n):
+        spread[j - 1].wait_send()
+        peer = lax.rem(me + n - j, n)
+        pltpu.make_async_remote_copy(
+            src_ref=pw_src,
+            dst_ref=pw_ref.at[peer],
+            send_sem=pw_send.at[j - 1],
+            recv_sem=pw_recv.at[j - 1],
+            device_id=(peer, g),
+            device_id_type=MESH,
+        ).wait_recv()
+    for k, j, copy in gathers:
         copy.wait_send()
         peer = lax.rem(me + n - j, n)
         pltpu.make_async_remote_copy(
-            src_ref=mine.at[k, pl.ds(0, size)],
-            dst_ref=out_ref.at[k, peer, pl.ds(0, size)],
+            src_ref=mine.at[k],
+            dst_ref=out_ref.at[k, peer],
             send_sem=ag_send.at[k, j - 1],
             recv_sem=ag_recv.at[k, j - 1],
             device_id=(peer, g),
@@ -180,27 +203,32 @@
     side = half // 2
     chunks = max(1, min(CHUNKS, half // (8 * n)))
     rows = half // (n * chunks)
-    blocks = max(1, cells // 1024)
+    blocks = max(1, cells // BLOCK)
     dma = pltpu.SemaphoreType.DMA
     f32, vmem = jnp.float32, pltpu.VMEM
     return pl.pallas_call(
         functools.partial(sum_kernel, n, m, chunks, blocks),
-        out_shape=jax.ShapeDtypeStruct((chunks, n, rows + EXTRA, half), f32),
+        out_shape=(
+            jax.ShapeDtypeStruct((chunks, n, rows, half), f32),
+            jax.ShapeDtypeStruct((n, 2, side), f32),
+        ),
         in_specs=[pl.BlockSpec(memory_space=pltpu.HBM)] * 2,
-        out_specs=pl.BlockSpec(memory_space=pltpu.VMEM),
+        out_specs=(pl.BlockSpec(memory_space=pltpu.VMEM),) * 2,
         scratch_shapes=[
             vmem((1, cells), jnp.int32),
             vmem((cells, width), jnp.bfloat16),
-            vmem((half + side, half), f32),
+            vmem((4 * side, half), f32),
+            vmem((side, width), f32),
             vmem((side, side), f32),
             vmem((half, half), f32),
             vmem((chunks, n - 1, rows, half), f32),
-            vmem((EXTRA, side), f32),
-            vmem((m - 1, EXTRA, side), f32),
-            vmem((chunks, rows + EXTRA, half), f32),
+            vmem((1, side), f32),
+            vmem((m - 1, 1, side), f32),
+            vmem((2, side), f32),
+            vmem((chunks, rows, half), f32),
             dma(()),
             dma((blocks,)),
-            [dma((chunks, n - 1)), dma((chunks, n - 1)), dma((m - 1,)), dma((m - 1,)), dma((chunks, n - 1)), dma((chunks, n - 1))],
+            [dma((chunks, n - 1)), dma((chunks, n - 1)), dma((m - 1,)), dma((m - 1,)), dma((n - 1,)), dma((n - 1,)), dma((chunks, n - 1)), dma((chunks, n - 1))],
         ],
         compiler_params=pltpu.CompilerParams(
             collective_id=0, has_side_effects=True, vmem_limit_bytes=VMEM_LIMIT
@@ -275,13 +303,11 @@
 
 
 def solve_kernel(
-    groups, block, parts_ref, dop_hbm, x_hbm, out_hbm,
+    groups, block, sum_ref, pw_ref, dop_hbm, x_hbm, out_hbm,
     dop, x_buf, out_buf, taps, re_parts, im_parts, pair, wide, xs, ys, acol, steer, w_ref,
     dop_sem, in_sems, out_sems,
 ):
-    chunks, n = parts_ref.shape[:2]
-    rows = parts_ref.shape[2] - EXTRA
-    half = parts_ref.shape[3]
+    half = sum_ref.shape[0]
     full = 2 * half
     bins = dop.shape[1]
     cells = x_buf.shape[0]
@@ -296,35 +322,39 @@
         copy.start()
         loads.append(copy)
 
-    summed = jnp.concatenate(
-        [parts_ref[k, j, :rows, :] for k in range(chunks) for j in range(n)], 0
-    )
-    power_row = parts_ref[chunks - 1, 0, rows:rows + 1, :half // 2]
-    for k in range(1, n):
-        power_row = power_row + parts_ref[chunks - 1, k, rows:rows + 1, :half // 2]
-    noise = jnp.sum(power_row, axis=1, keepdims=True) / (groups * half)
-    low = load_ratio * noise
-    r = lax.broadcasted_iota(jnp.int32, (half, half), 0)
-    c = lax.broadcasted_iota(jnp.int32, (half, half), 1)
-    trace = total(jnp.where(r == c, summed, 0.0))
-    unit = 1.0 / (trace + low)
-    norm = summed * unit
-    norm = norm * norm
-    fro = jnp.sqrt(total(jnp.where(r == c, norm, norm + norm))) * (trace + low)
-    bound = jnp.minimum(trace, 1.0001 * fro)
+    power = pw_ref[0]
+    for k in range(1, pw_ref.shape[0]):
+        power = power + pw_ref[k]
+    power = jnp.sum(power, axis=1, keepdims=True)
+    low = (load_ratio / (groups * half)) * power[:1]
+    bound = 1.0001 * power[1:]
     scale = 2.0 / (bound + 2.0 * low)
+    side = half // 2
+    r = lax.broadcasted_iota(jnp.int32, (side, side), 0)
+    c = lax.broadcasted_iota(jnp.int32, (side, side), 1)
     eye = jnp.where(r == c, 1.0, 0.0)
-    flip = summed.T
-    real = (jnp.where(r <= c, summed, flip) + low * eye) * scale
-    imag = jnp.where(r > c, summed, jnp.where(r < c, -flip, 0.0)) * scale
-    acol[:half, :] = real
-    acol[half:, :] = imag
-    for k, (xr, xi) in enumerate(zip(split(real, 3), split(imag, 3))):
-        re_parts[k * half:(k + 1) * half, :] = xr
-        im_parts[k * half:(k + 1) * half, :] = xi
-        if k == 0:
-            pair[:half, :] = xr
-            pair[half:full, :] = xi
+
+    def put(i, j, xr, xi):
+        at, to = slice(i * side, (i + 1) * side), slice(j * side, (j + 1) * side)
+        acol[at, to] = xr
+        acol[half + i * side:half + (i + 1) * side, to] = xi
+        for k, (tr, ti) in enumerate(zip(split(xr, 3), split(xi, 3))):
+            re_parts[k * half + i * side:k * half + (i + 1) * side, to] = tr
+            im_parts[k * half + i * side:k * half + (i + 1) * side, to] = ti
+            if k == 0:
+                pair[at, to] = tr
+                pair[half + i * side:half + (i + 1) * side, to] = ti
+
+    for i in range(2):
+        own = sum_ref[i * side:(i + 1) * side, i * side:(i + 1) * side]
+        flip = own.T
+        xr = (jnp.where(r <= c, own, flip) + low * eye) * scale
+        xi = jnp.where(r > c, own, jnp.where(r < c, -flip, 0.0)) * scale
+        put(i, i, xr, xi)
+    upper = sum_ref[:side, side:] * scale
+    lower = sum_ref[side:, :side] * scale
+    put(0, 1, upper, -lower.T)
+    put(1, 0, upper.T, lower)
 
     def times(left, re, im):
         rows = left.shape[0] // 2
@@ -351,7 +381,10 @@
         bend = bend_of(d)
         a = acol[...] * (bend * gainup)
         x1 = -a
-        xs[...] = jnp.concatenate([x1[:half] + (2.0 * bend) * eye, x1[half:]], 0)
+        xs[...] = x1
+        for i in range(2):
+            at = slice(i * side, (i + 1) * side)
+            xs[at, at] = x1[at, at] + (2.0 * bend) * eye
         ys[...] = 2.0 * a - square * (bend * gainup * gainup)
         return grow(d)
 
@@ -470,11 +503,14 @@
 START = [start_for(k, GOAL) for k in range(12)]
 COARSE = 0.005
 CHUNKS = 2
+DEPTH = 8
+BLOCK = 2048
+WIDE = 4096
 VMEM_LIMIT = 52 * 1024 * 1024
 
 
-def solve(parts, doppler, snaps, groups, block):
-    half = parts.shape[3]
+def solve(summed, power, doppler, snaps, groups, block):
+    half = summed.shape[0]
     bins = doppler.shape[1]
     cells, width = snaps.shape
     full = 2 * half
@@ -485,6 +521,7 @@
         functools.partial(solve_kernel, groups, block),
         out_shape=jax.ShapeDtypeStruct((2 * bins, cells), bf16),
         in_specs=[
+            pl.BlockSpec(memory_space=pltpu.VMEM),
             pl.BlockSpec(memory_space=pltpu.VMEM),
             pl.BlockSpec(memory_space=pltpu.HBM),
             pl.BlockSpec(memory_space=pltpu.HBM),
@@ -510,13 +547,16 @@
         ],
         compiler_params=pltpu.CompilerParams(vmem_limit_bytes=VMEM_LIMIT),
         name="solve",
-    )(parts, doppler, snaps)
+    )(summed, power, doppler, snaps)
 
 
 def per_device(snapshots, training, doppler):
     snaps = snapshots[0]
-    parts = gram_sum(snaps, training[None, :])
-    return solve(parts, doppler, snaps, lax.axis_size("bins"), 1024)[None]
+    keep = pltpu.with_memory_space_constraint(training[None, :], pltpu.HBM)
+    parts, power = gram_sum(snaps, keep)
+    half = parts.shape[3]
+    summed = parts.reshape(half, half)
+    return solve(summed, power, doppler, snaps, lax.axis_size("bins"), 1024)[None]
 
 
 def solution(mesh):

time: 33 us -> 32.5 us (0.985)
  local copies, waits for them, and re-layouts: 0.77 us -> 0.01 us
  Pallas kernels: 31.5 us -> 32.1 us
    unnamed x4 -> x2, local copies, waits for them, and re-layouts: 0.77 us -> 0.01 us
    pallas_call x1, Pallas kernels: 7.98 us -> 8.32 us  [solve(): pl.pallas_call(functools.partial(solve_kernel, groups, block), out_shape=...]
where the time goes in v3:
time: 32.5 us; the launch traced here: 32.1 us
  Pallas kernels  32.1 us (99%)
    pallas_call x1, Pallas kernels, gram_sum(): pl.pallas_call(functools.partial(sum_kernel, n, m, chunks, blocks), out_s...  23.8 us
    pallas_call x1, Pallas kernels, solve(): pl.pallas_call(functools.partial(solve_kernel, groups, block), out_shape=...  8.32 us

profile of v3, /device:TPU:0, one launch (start us, length us, event | category | flops | bytes accessed | tf_op | source)
XLA Modules:
  0.0 32.1 jit_solution(1062978660009628177)
XLA Ops:
  0.0 0.0 copy-start
  0.0 23.8 %gram_sum.1 = (f32[2,8,16,256]{3,2,1,0:T(8,128)S(1)}, f32[8,2,128]{2,1,0:T(2,128)S(1)}) custom-call(s32[1,8192]{1,0:T(1,128)} %bitcast.7, bf16[8192,512]{1,0:T(8,128)(2,1)} %bitcast.5), custom_call_target="tpu_custom_call" | custom-call | tf_op jit(solution)/shard_map/gram_sum/pallas_call | solution.py:209
  23.8 0.0 copy-done
  23.8 8.3 %solve.1 = bf16[256,8192]{1,0:T(8,128)(2,1)} custom-call(f32[256,256]{1,0:T(8,128)S(1)} %bitcast.4, f32[8,2,128]{2,1,0:T(2,128)S(1)} %get-tuple-element.8.pw_ref, s32[1,128]{1,0:T(1,128)S(1)} %copy-done, bf16[8192,512]{1,0:T(8,128)(2,1)} %bitcast.6), custom_call_target="tpu_custom_call" | custom-call | tf_op jit(solution)/shard_map/solve/pallas_call | solution.py:520
Async XLA Ops:
  0.0 23.8 %copy-start = (s32[1,128]{1,0:T(1,128)S(1)}, s32[1,128]{1,0:T(1,128)}, u32[]{:S(2)}) copy-start(s32[1,128]{1,0:T(1,128)} %dop_hbm.1) | copy-start | bytes 1540

commit v4 on v3

--- a/solution.py
+++ b/solution.py
@@ -33,11 +33,11 @@
     rs_send, rs_recv, tr_send, tr_recv, pw_send, pw_recv, ag_send, ag_recv = sems
     block = cells // blocks
 
+    keep_copy = pltpu.make_async_copy(keep_hbm, keep_ref, keep_sem)
+    keep_copy.start()
     for k in range(min(DEPTH, blocks)):
         span = pl.ds(k * block, block)
         pltpu.make_async_copy(x_hbm.at[span], x_buf.at[span], in_sems.at[k]).start()
-    keep_copy = pltpu.make_async_copy(keep_hbm, keep_ref, keep_sem)
-    keep_copy.start()
     barrier = pltpu.get_barrier_semaphore()
     for k in range(1, n):
         pl.semaphore_signal(
@@ -503,9 +503,9 @@
 START = [start_for(k, GOAL) for k in range(12)]
 COARSE = 0.005
 CHUNKS = 2
-DEPTH = 8
+DEPTH = 2
 BLOCK = 2048
-WIDE = 4096
+WIDE = 2048
 VMEM_LIMIT = 52 * 1024 * 1024
 
 

time: 32.5 us -> 30.7 us (0.945)
  Pallas kernels: 32.1 us -> 30.5 us
    pallas_call x1, Pallas kernels: 23.8 us -> 22.2 us  [gram_sum(): pl.pallas_call(functools.partial(sum_kernel, n, m, chunks, blocks), out_s...]
where the time goes in v4:
time: 30.7 us; the launch traced here: 30.6 us
  Pallas kernels  30.5 us (99%)
    pallas_call x1, Pallas kernels, gram_sum(): pl.pallas_call(functools.partial(sum_kernel, n, m, chunks, blocks), out_s...  22.2 us
    pallas_call x1, Pallas kernels, solve(): pl.pallas_call(functools.partial(solve_kernel, groups, block), out_shape=...  8.31 us

profile of v4, /device:TPU:0, one launch (start us, length us, event | category | flops | bytes accessed | tf_op | source)
XLA Modules:
  0.0 30.6 jit_solution(1091587663287041804)
XLA Ops:
  0.0 0.0 copy-start
  0.0 22.2 %gram_sum.1 = (f32[2,8,16,256]{3,2,1,0:T(8,128)S(1)}, f32[8,2,128]{2,1,0:T(2,128)S(1)}) custom-call(s32[1,8192]{1,0:T(1,128)} %bitcast.7, bf16[8192,512]{1,0:T(8,128)(2,1)} %bitcast.5), custom_call_target="tpu_custom_call" | custom-call | tf_op jit(solution)/shard_map/gram_sum/pallas_call | solution.py:209
  22.2 0.0 copy-done
  22.2 8.3 %solve.1 = bf16[256,8192]{1,0:T(8,128)(2,1)} custom-call(f32[256,256]{1,0:T(8,128)S(1)} %bitcast.4, f32[8,2,128]{2,1,0:T(2,128)S(1)} %get-tuple-element.8.pw_ref, s32[1,128]{1,0:T(1,128)S(1)} %copy-done, bf16[8192,512]{1,0:T(8,128)(2,1)} %bitcast.6), custom_call_target="tpu_custom_call" | custom-call | tf_op jit(solution)/shard_map/solve/pallas_call | solution.py:520
Async XLA Ops:
  0.0 22.2 %copy-start = (s32[1,128]{1,0:T(1,128)S(1)}, s32[1,128]{1,0:T(1,128)}, u32[]{:S(2)}) copy-start(s32[1,128]{1,0:T(1,128)} %dop_hbm.1) | copy-start | bytes 1540
